TPU v7x, 32 devices: a whole 2x2x4 slice. The times are simulated.
32 devices in a mesh: dp: 4 (over z), row: 2 (over x), col: 4 (over y, core).
Axes of the slice: x: 2, y: 2, z: 4, core: 2. Of those that a mesh axis runs over, the one named last changes fastest.
Arguments:
- inputs: bfloat16 [4096, 1536], P(('dp', 'row'), 'col'), may hold values from -12.5 to 12.5
- gain_attn: bfloat16 [1536], P(('col', 'dp')), may hold values from 0.25 to 1.75
- w_query: bfloat16 [1536, 1536], P(('col', 'dp'), 'row'), may hold values from -0.15625 to 0.15625
- b_query: bfloat16 [1536], P(('row', 'dp')), may hold values from -3 to 3
- key_weight: bfloat16 [1536, 256], P(('col', 'dp'), 'row'), may hold values from -0.15625 to 0.15625
- key_bias: bfloat16 [256], P(('row', 'dp')), may hold values from -3 to 3
- value_weight: bfloat16 [1536, 256], P(('col', 'dp'), 'row'), may hold values from -0.15625 to 0.15625
- value_bias: bfloat16 [256], P(('row', 'dp')), may hold values from -3 to 3
- w_output: bfloat16 [1536, 1536], P(('row', 'dp'), 'col'), may hold values from -1.25 to 1.25
- gain_mlp: bfloat16 [1536], P(('col', 'dp')), may hold values from 0.25 to 1.75
- w_gate: bfloat16 [1536, 8960], P(('col', 'dp'), 'row'), may hold values from -0.15625 to 0.15625
- w_up: bfloat16 [1536, 8960], P(('col', 'dp'), 'row'), may hold values from -0.15625 to 0.15625
- w_down: bfloat16 [8960, 1536], P(('row', 'dp'), 'col'), may hold values from -0.0625 to 0.0625
- cotangent: bfloat16 [4096, 1536], P(('dp', 'row'), 'col'), may hold values from -6 to 6
Outputs:
- outputs: bfloat16 [4096, 1536], P(('dp', 'row'), 'col')
- grad_inputs: bfloat16 [4096, 1536], P(('dp', 'row'), 'col')
- grad_gain_attn: float32 [1536], P(('col', 'dp'))
- grad_w_query: float32 [1536, 1536], P(('col', 'dp'), 'row')
- grad_b_query: float32 [1536], P(('row', 'dp'))
- grad_w_key: float32 [1536, 256], P(('col', 'dp'), 'row')
- grad_b_key: float32 [256], P(('row', 'dp'))
- grad_w_value: float32 [1536, 256], P(('col', 'dp'), 'row')
- grad_b_value: float32 [256], P(('row', 'dp'))
- grad_w_output: float32 [1536, 1536], P(('row', 'dp'), 'col')
- grad_gain_mlp: float32 [1536], P(('col', 'dp'))
- grad_w_gate: float32 [1536, 8960], P(('col', 'dp'), 'row')
- grad_w_up: float32 [1536, 8960], P(('col', 'dp'), 'row')
- grad_w_down: float32 [8960, 1536], P(('row', 'dp'), 'col')
All inputs are finite; a program needn't handle non-finite values.
Results may differ from a plain program's by a relative error of at most 0.025.
Values may be sent and summed in bfloat16 or wider, within the bound.
A program may use at most 256 MiB of HBM per device.

v0:
```python
import jax
import jax.numpy as jnp
from jax import lax
from jax.sharding import PartitionSpec as P

MODEL_WIDTH = 1536
HEAD_SIZE = 128
epsilon = 1e-06
rope_base = 1000000.0


def shortened(shard):
    return jax.tree.map(lambda a: a.astype(jnp.bfloat16) if a.dtype == jnp.float32 else a, shard)


def rope_turn(value_rows, positions, direction):
    row_count = value_rows.shape[0]
    heads = value_rows.shape[1] // HEAD_SIZE
    half = HEAD_SIZE // 2
    freqs = rope_base ** (-(jnp.arange(half, dtype=jnp.float32) * 2.0 / HEAD_SIZE))
    angles = positions.astype(jnp.float32)[:, None] * freqs[None, :]
    cosine = jnp.cos(angles)[:, None, :]
    sine = direction * jnp.sin(angles)[:, None, :]
    shaped = value_rows.reshape(row_count, heads, HEAD_SIZE)
    first = shaped[..., :half]
    second = shaped[..., half:]
    turned = jnp.concatenate([first * cosine - second * sine, second * cosine + first * sine], -1)
    return turned.reshape(row_count, heads * HEAD_SIZE)


def outer_sum(left, right):
    return lax.dot_general(
        left, right, (((0,), (0,)), ((), ())), preferred_element_type=jnp.float32
    )


def back_product(left, weight):
    return lax.dot_general(
        left, weight, (((1,), (1,)), ((), ())), preferred_element_type=jnp.float32
    )


def norm_forward(value_rows, gain):
    squares = lax.psum(jnp.sum(value_rows * value_rows, axis=1), "col")
    inv_rms = lax.rsqrt(squares / MODEL_WIDTH + epsilon)[:, None]
    return (value_rows * inv_rms * gain.astype(jnp.float32), inv_rms)


def norm_backward(value_rows, inv_rms, gain, grad_in):
    weighted = grad_in * gain.astype(jnp.float32)
    inner = lax.psum(jnp.sum(weighted * value_rows, axis=1), "col")[:, None]
    return inv_rms * weighted - value_rows * inv_rms * inv_rms * inv_rms * inner / MODEL_WIDTH


def rows_whole(local):
    return lax.all_gather(local, "row", axis=0, tiled=True)


def cols_whole(local):
    return jax.tree.map(
        lambda part, own: part.astype(own.dtype),
        lax.all_gather(shortened(local), "col", axis=0, tiled=True),
        local,
    )


def rows_sum(term):
    return lax.psum_scatter(term, "row", scatter_dimension=0, tiled=True)


def width_sum(whole, weight, contract):

    def term(first_row, row_count):
        return lax.dot_general(
            whole, weight, (((1,), (contract,)), ((), ())), preferred_element_type=jnp.float32
        )

    return lax.psum_scatter(
        term(jnp.int32(0), lax.axis_size("col") * (whole.shape[0] // lax.axis_size("col"))),
        "col",
        scatter_dimension=0,
        tiled=True,
    )


def score_block(query_rows, keys_all, positions):
    rows_per_block = query_rows.shape[0]
    kv_heads = keys_all.shape[1] // HEAD_SIZE
    heads_per_group = query_rows.shape[1] // HEAD_SIZE // kv_heads
    query_four = query_rows.reshape(rows_per_block, kv_heads, heads_per_group, HEAD_SIZE)
    keys_triple_shape = keys_all.reshape(keys_all.shape[0], kv_heads, HEAD_SIZE)
    scores = jnp.einsum(
        "ikgd,jkd->kgij", query_four, keys_triple_shape, preferred_element_type=jnp.float32
    ) * HEAD_SIZE ** (-0.5)
    admitted = jnp.arange(keys_all.shape[0], dtype=jnp.int32)[None, :] <= positions[:, None]
    return (jnp.where(admitted, scores, -1e30), query_four, keys_triple_shape)


def attend_forward(query_rows, keys_all, values_all, positions):
    scores, query_four, keys_triple_shape = score_block(query_rows, keys_all, positions)
    top_score = jnp.max(scores, axis=-1, keepdims=True)
    expo = jnp.exp(scores - top_score)
    totals = jnp.sum(expo, axis=-1, keepdims=True)
    probs = (expo / totals).astype(jnp.bfloat16)
    log_total = (top_score + jnp.log(totals))[..., 0]
    values_triple_shape = values_all.reshape(keys_triple_shape.shape)
    attended = jnp.einsum(
        "kgij,jkd->ikgd", probs, values_triple_shape, preferred_element_type=jnp.float32
    )
    return (attended.reshape(query_rows.shape).astype(jnp.bfloat16), log_total)


def attend_backward(query_rows, keys_all, values_all, positions, log_total, d_attended):
    scores, query_four, keys_triple_shape = score_block(query_rows, keys_all, positions)
    probs = jnp.exp(scores - log_total[..., None])
    probs_low = probs.astype(jnp.bfloat16)
    values_triple_shape = values_all.reshape(keys_triple_shape.shape)
    grad_four = d_attended.reshape(query_four.shape)
    d_probs = jnp.einsum(
        "ikgd,jkd->kgij", grad_four, values_triple_shape, preferred_element_type=jnp.float32
    )
    centre = jnp.sum(probs * d_probs, axis=-1, keepdims=True)
    d_scores = (probs * (d_probs - centre)).astype(jnp.bfloat16)
    d_queries = jnp.einsum(
        "kgij,jkd->ikgd", d_scores, keys_triple_shape, preferred_element_type=jnp.float32
    )
    d_keys = jnp.einsum("kgij,ikgd->jkd", d_scores, query_four, preferred_element_type=jnp.float32)
    d_values = jnp.einsum(
        "kgij,ikgd->jkd", probs_low, grad_four, preferred_element_type=jnp.float32
    )
    scale_factor = HEAD_SIZE ** (-0.5)
    return (
        d_queries.reshape(query_rows.shape) * scale_factor,
        d_keys.reshape(keys_all.shape) * scale_factor,
        d_values.reshape(values_all.shape),
    )


def shards(
    inputs,
    gain_attn,
    w_query,
    b_query,
    key_weight,
    key_bias,
    value_weight,
    value_bias,
    w_output,
    gain_mlp,
    w_gate,
    w_up,
    w_down,
    cotangent,
):
    (
        gain_attn,
        w_query,
        b_query,
        key_weight,
        key_bias,
        value_weight,
        value_bias,
        w_output,
        gain_mlp,
        w_gate,
        w_up,
        w_down,
    ) = (
        lax.all_gather(gain_attn, "dp", axis=0, tiled=True),
        lax.all_gather(w_query, "dp", axis=0, tiled=True),
        lax.all_gather(b_query, "dp", axis=0, tiled=True),
        lax.all_gather(key_weight, "dp", axis=0, tiled=True),
        lax.all_gather(key_bias, "dp", axis=0, tiled=True),
        lax.all_gather(value_weight, "dp", axis=0, tiled=True),
        lax.all_gather(value_bias, "dp", axis=0, tiled=True),
        lax.all_gather(w_output, "dp", axis=0, tiled=True),
        lax.all_gather(gain_mlp, "dp", axis=0, tiled=True),
        lax.all_gather(w_gate, "dp", axis=0, tiled=True),
        lax.all_gather(w_up, "dp", axis=0, tiled=True),
        lax.all_gather(w_down, "dp", axis=0, tiled=True),
    )
    local_rows = inputs.shape[0]
    seq_len = local_rows * lax.axis_size("row")
    rows_per_block = seq_len // lax.axis_size("col")
    positions = lax.axis_index("col") * rows_per_block + jnp.arange(rows_per_block, dtype=jnp.int32)
    width_q = w_query.shape[1]
    width_kv = key_weight.shape[1]
    units = w_gate.shape[1]
    inputs_wide = inputs.astype(jnp.float32)
    normed1, inv_rms1 = norm_forward(inputs_wide, gain_attn)
    normed1_all = rows_whole(normed1.astype(jnp.bfloat16))
    projected = width_sum(normed1_all, jnp.concatenate([w_query, key_weight, value_weight], 1), 0)
    projected = projected + jnp.concatenate([b_query, key_bias, value_bias]).astype(jnp.float32)
    query_rows = rope_turn(projected[:, :width_q], positions, 1.0).astype(jnp.bfloat16)
    rotated_keys = rope_turn(projected[:, width_q : width_q + width_kv], positions, 1.0).astype(
        jnp.bfloat16
    )
    value_rows = projected[:, width_q + width_kv :].astype(jnp.bfloat16)
    keys_all, values_all = (
        lax.all_gather(rotated_keys, "col", axis=0, tiled=True),
        lax.all_gather(value_rows, "col", axis=0, tiled=True),
    )
    attended, log_total = attend_forward(query_rows, keys_all, values_all, positions)
    attended_all = cols_whole(attended)
    middle = inputs_wide + rows_sum(
        jnp.dot(attended_all, w_output, preferred_element_type=jnp.float32)
    )
    normed2, inv_rms2 = norm_forward(middle, gain_mlp)
    normed2_all = rows_whole(normed2.astype(jnp.bfloat16))
    both_pre = width_sum(normed2_all, jnp.concatenate([w_gate, w_up], 1), 0)
    gate_pre = both_pre[:, :units]
    up_pre = both_pre[:, units:]
    sigmoid_gate = jax.nn.sigmoid(gate_pre)
    silu_gate = gate_pre * sigmoid_gate
    hidden = (silu_gate * up_pre).astype(jnp.bfloat16)
    hidden_all = cols_whole(hidden)
    outputs = middle + rows_sum(jnp.dot(hidden_all, w_down, preferred_element_type=jnp.float32))
    cot_all = rows_whole(cotangent)
    grad_down = outer_sum(hidden_all, cot_all)
    d_hidden = width_sum(cot_all, w_down, 1)
    d_gate = (d_hidden * up_pre * sigmoid_gate * (1.0 + gate_pre * (1.0 - sigmoid_gate))).astype(
        jnp.bfloat16
    )
    d_up = (d_hidden * silu_gate).astype(jnp.bfloat16)
    d_gate_all, d_up_all = cols_whole((d_gate, d_up))
    grad_gate = outer_sum(normed2_all, d_gate_all)
    grad_up = outer_sum(normed2_all, d_up_all)
    d_norm2 = rows_sum(back_product(d_gate_all, w_gate) + back_product(d_up_all, w_up))
    d_middle = cotangent.astype(jnp.float32) + norm_backward(middle, inv_rms2, gain_mlp, d_norm2)
    d_middle_all = rows_whole(d_middle.astype(jnp.bfloat16))
    grad_output = outer_sum(attended_all, d_middle_all)
    d_attended = width_sum(d_middle_all, w_output, 1).astype(jnp.bfloat16)
    d_queries, d_keys_part, d_values_part = attend_backward(
        query_rows, keys_all, values_all, positions, log_total, d_attended
    )
    d_keys, d_values = (
        lax.psum_scatter(d_keys_part, "col", scatter_dimension=0, tiled=True),
        lax.psum_scatter(d_values_part, "col", scatter_dimension=0, tiled=True),
    )
    d_query_low = rope_turn(d_queries, positions, -1.0).astype(jnp.bfloat16)
    d_key_low = rope_turn(d_keys, positions, -1.0).astype(jnp.bfloat16)
    d_value_low = d_values.astype(jnp.bfloat16)
    d_query_all, d_key_all, d_value_all = cols_whole((d_query_low, d_key_low, d_value_low))
    grad_query = outer_sum(normed1_all, d_query_all)
    grad_key = outer_sum(normed1_all, d_key_all)
    grad_value = outer_sum(normed1_all, d_value_all)
    grad_bias_q = jnp.sum(d_query_all, axis=0, dtype=jnp.float32)
    grad_bias_k = jnp.sum(d_key_all, axis=0, dtype=jnp.float32)
    grad_bias_v = jnp.sum(d_value_all, axis=0, dtype=jnp.float32)
    d_norm1 = rows_sum(
        back_product(d_query_all, w_query)
        + back_product(d_key_all, key_weight)
        + back_product(d_value_all, value_weight)
    )
    grad_inputs = d_middle + norm_backward(inputs_wide, inv_rms1, gain_attn, d_norm1)
    gain_term1 = jnp.sum(d_norm1 * inputs_wide * inv_rms1, axis=0)
    gain_term2 = jnp.sum(d_norm2 * middle * inv_rms2, axis=0)
    gain_sum1, gain_sum2 = lax.psum((gain_term1, gain_term2), "row")
    summed = (
        lax.psum_scatter(
            gain_sum1.astype(jnp.bfloat16), "dp", scatter_dimension=0, tiled=True
        ).astype(jnp.float32),
        lax.psum_scatter(
            grad_query.astype(jnp.bfloat16), "dp", scatter_dimension=0, tiled=True
        ).astype(jnp.float32),
        lax.psum_scatter(
            grad_bias_q.astype(jnp.bfloat16), "dp", scatter_dimension=0, tiled=True
        ).astype(jnp.float32),
        lax.psum_scatter(
            grad_key.astype(jnp.bfloat16), "dp", scatter_dimension=0, tiled=True
        ).astype(jnp.float32),
        lax.psum_scatter(
            grad_bias_k.astype(jnp.bfloat16), "dp", scatter_dimension=0, tiled=True
        ).astype(jnp.float32),
        lax.psum_scatter(
            grad_value.astype(jnp.bfloat16), "dp", scatter_dimension=0, tiled=True
        ).astype(jnp.float32),
        lax.psum_scatter(
            grad_bias_v.astype(jnp.bfloat16), "dp", scatter_dimension=0, tiled=True
        ).astype(jnp.float32),
        lax.psum_scatter(
            grad_output.astype(jnp.bfloat16), "dp", scatter_dimension=0, tiled=True
        ).astype(jnp.float32),
        lax.psum_scatter(
            gain_sum2.astype(jnp.bfloat16), "dp", scatter_dimension=0, tiled=True
        ).astype(jnp.float32),
        lax.psum_scatter(
            grad_gate.astype(jnp.bfloat16), "dp", scatter_dimension=0, tiled=True
        ).astype(jnp.float32),
        lax.psum_scatter(
            grad_up.astype(jnp.bfloat16), "dp", scatter_dimension=0, tiled=True
        ).astype(jnp.float32),
        lax.psum_scatter(
            grad_down.astype(jnp.bfloat16), "dp", scatter_dimension=0, tiled=True
        ).astype(jnp.float32),
    )
    return (outputs.astype(jnp.bfloat16), grad_inputs.astype(jnp.bfloat16)) + tuple(summed)


def solution(mesh):
    return jax.shard_map(
        shards,
        mesh=mesh,
        in_specs=(
            P(("dp", "row"), "col"),
            P(("col", "dp")),
            P(("col", "dp"), "row"),
            P(("row", "dp")),
            P(("col", "dp"), "row"),
            P(("row", "dp")),
            P(("col", "dp"), "row"),
            P(("row", "dp")),
            P(("row", "dp"), "col"),
            P(("col", "dp")),
            P(("col", "dp"), "row"),
            P(("col", "dp"), "row"),
            P(("row", "dp"), "col"),
            P(("dp", "row"), "col"),
        ),
        out_specs=(
            P(("dp", "row"), "col"),
            P(("dp", "row"), "col"),
            P(("col", "dp")),
            P(("col", "dp"), "row"),
            P(("row", "dp")),
            P(("col", "dp"), "row"),
            P(("row", "dp")),
            P(("col", "dp"), "row"),
            P(("row", "dp")),
            P(("row", "dp"), "col"),
            P(("col", "dp")),
            P(("col", "dp"), "row"),
            P(("col", "dp"), "row"),
            P(("row", "dp"), "col"),
        ),
        check_vma=False,
    )
```

profile of v0, /device:TPU:0, one launch (start us, length us, event | category | flops | bytes accessed | tf_op | source)
XLA Modules:
  0.0 1542.8 jit_solution(1339654693611633211)
XLA Ops:
  48.0 16.3 %all_gather.77 = bf16[384,768]{1,0:T(8,128)(2,1)S(1)} all-gather(bf16[96,768]{1,0:T(8,128)(2,1)} %param.16), channel_id=1, replica_groups=mesh['dp'=4,'row'=2,'col'=4] {'dp'}, dimensions={0}, use_global_device_ids=true | all-gather | bytes 737280 | tf_op jit(solution)/shard_map/all_gather | solution.py:170
  96.2 41.1 %reduce-scatter.18.cloned.1.call-done = f32[256,1024]{0,1:T(8,128)} async-done(((f32[1024,1024]{0,1:T(8,128)}), f32[256,1024]{0,1:T(8,128)}) %reduce-scatter.18.cloned.1.call-update) | async-done | bytes 1048592 | tf_op jit(solution)/shard_map/reduce_scatter | solution.py:78
  157.5 17.3 %all_gather.86 = bf16[768,384]{1,0:T(8,128)(2,1)S(1)} all-gather(bf16[192,384]{1,0:T(8,128)(2,1)S(1)} %copy-done.25), channel_id=1, replica_groups=mesh['dp'=4,'row'=2,'col'=4] {'dp'}, dimensions={0}, use_global_device_ids=true | all-gather | bytes 737280 | tf_op jit(solution)/shard_map/all_gather | solution.py:176
  193.9 52.7 %all-gather.19.cloned.1.call-done = bf16[4480,384]{1,0:T(8,128)(2,1)} async-done(((bf16[1120,384]{1,0:T(8,128)(2,1)}), bf16[4480,384]{1,0:T(8,128)(2,1)}) %all-gather.19.cloned.1.call-update) | async-done | bytes 3440656 | tf_op jit(solution)/shard_map/all_gather | solution.py:180
  257.6 16.4 %reduce-scatter.20.cloned.1.call-done = f32[512,384]{1,0:T(8,128)} async-done(((f32[1024,384]{1,0:T(8,128)}), f32[512,384]{1,0:T(8,128)}) %reduce-scatter.20.cloned.1.call-update) | async-done | bytes 786448 | tf_op jit(solution)/shard_map/reduce_scatter | solution.py:68
  292.7 51.1 %all-gather.13.cloned.1.call-done = bf16[384,4480]{1,0:T(8,128)(2,1)} async-done(((bf16[96,4480]{1,0:T(8,128)(2,1)}), bf16[384,4480]{1,0:T(8,128)(2,1)}) %all-gather.13.cloned.1.call-update) | async-done | bytes 3440656 | tf_op jit(solution)/shard_map/all_gather | solution.py:178
  343.8 68.4 %all-gather.15.cloned.1.call-done = bf16[384,4480]{1,0:T(8,128)(2,1)} async-done(((bf16[96,4480]{1,0:T(8,128)(2,1)}), bf16[384,4480]{1,0:T(8,128)(2,1)}) %all-gather.15.cloned.1.call-update) | async-done | bytes 3440656 | tf_op jit(solution)/shard_map/all_gather | solution.py:179
  412.2 26.8 %fusion = f32[1024,8960]{1,0:T(8,128)} fusion(bf16[1024,384]{1,0:T(8,128)(2,1)S(1)} %all_gather.88, bf16[384,4480]{1,0:T(8,128)(2,1)} %all-gather.15.cloned.1.call-done, bf16[384,4480]{1,0:T(8,128)(2,1)} %all-gather.13.cloned.1.call-done), kind=kOutput, calls=%fused_computation.3 | convolution fusion | flops 7060193280 | bytes 44367872 | tf_op jit(solution)/shard_map/dot_general | solution.py:74
  439.1 109.0 %reduce-scatter.26.cloned.1.call-done = f32[256,4480]{1,0:T(8,128)} async-done(((f32[1024,4480]{1,0:T(8,128)}), f32[256,4480]{1,0:T(8,128)}) %reduce-scatter.26.cloned.1.call-update) | async-done | bytes 4587536 | tf_op jit(solution)/shard_map/reduce_scatter | solution.py:78
  548.0 253.9 %reduce-scatter.22.cloned.1.call-done = f32[256,8960]{1,0:T(8,128)} async-done(((f32[1024,8960]{1,0:T(8,128)}), f32[256,8960]{1,0:T(8,128)}) %reduce-scatter.22.cloned.1.call-update) | async-done | bytes 9175056 | tf_op jit(solution)/shard_map/reduce_scatter | solution.py:78
  811.1 61.5 %all-gather.21.cloned.1.call-done = bf16[1024,4480]{1,0:T(8,128)(2,1)} async-done(((bf16[256,4480]{1,0:T(8,128)(2,1)}), bf16[1024,4480]{1,0:T(8,128)(2,1)}) %all-gather.21.cloned.1.call-update) | async-done | bytes 9175056 | tf_op jit(solution)/shard_map/all_gather | solution.py:62
  882.0 54.8 %all-gather.23.cloned.1.call-done = bf16[1024,4480]{1,0:T(8,128)(2,1)} async-done(((bf16[256,4480]{1,0:T(8,128)(2,1)}), bf16[1024,4480]{1,0:T(8,128)(2,1)}) %all-gather.23.cloned.1.call-update) | async-done | bytes 9175056 | tf_op jit(solution)/shard_map/all_gather | solution.py:62
  946.5 54.6 %all-gather.17.cloned.1.call-done = bf16[1024,4480]{1,0:T(8,128)(2,1)} async-done(((bf16[256,4480]{1,0:T(8,128)(2,1)}), bf16[1024,4480]{1,0:T(8,128)(2,1)}) %all-gather.17.cloned.1.call-update) | async-done | bytes 9175056 | tf_op jit(solution)/shard_map/all_gather | solution.py:62
  1010.5 19.4 %reduce-scatter.28.cloned.1.call-done = f32[512,384]{1,0:T(8,128)} async-done(((f32[1024,384]{1,0:T(8,128)}), f32[512,384]{1,0:T(8,128)}) %reduce-scatter.28.cloned.1.call-update) | async-done | bytes 786448 | tf_op jit(solution)/shard_map/reduce_scatter | solution.py:68
  1038.5 20.4 %reduce-scatter.24.cloned.1.call-done = f32[512,384]{1,0:T(8,128)} async-done(((f32[1024,384]{1,0:T(8,128)}), f32[512,384]{1,0:T(8,128)}) %reduce-scatter.24.cloned.1.call-update) | async-done | bytes 786448 | tf_op jit(solution)/shard_map/reduce_scatter | solution.py:68
  1076.8 38.0 %reduce-scatter.30.cloned.1.call-done = f32[256,768]{1,0:T(8,128)} async-done(((f32[1024,768]{1,0:T(8,128)}), f32[256,768]{1,0:T(8,128)}) %reduce-scatter.30.cloned.1.call-update) | async-done | bytes 786448 | tf_op jit(solution)/shard_map/reduce_scatter | solution.py:78
  1200.3 15.2 reduce-scatter.44.cloned.1.call-done
  1217.1 64.1 %reduce-scatter.48.cloned.1.call-done = bf16[96,4480]{1,0:T(8,128)(2,1)} async-done(((bf16[384,4480]{1,0:T(8,128)(2,1)}), bf16[96,4480]{1,0:T(8,128)(2,1)}) %reduce-scatter.48.cloned.1.call-update) | async-done | bytes 860176 | tf_op jit(solution)/shard_map/reduce_scatter | solution.py:290
  1283.6 64.8 %reduce-scatter.46.cloned.1.call-done = bf16[96,4480]{1,0:T(8,128)(2,1)} async-done(((bf16[384,4480]{1,0:T(8,128)(2,1)}), bf16[96,4480]{1,0:T(8,128)(2,1)}) %reduce-scatter.46.cloned.1.call-update) | async-done | bytes 860176 | tf_op jit(solution)/shard_map/reduce_scatter | solution.py:287
  1351.0 65.0 %reduce-scatter.50.cloned.1.call-done = bf16[1120,384]{1,0:T(8,128)(2,1)} async-done(((bf16[4480,384]{1,0:T(8,128)(2,1)}), bf16[1120,384]{1,0:T(8,128)(2,1)}) %reduce-scatter.50.cloned.1.call-update) | async-done | bytes 860176 | tf_op jit(solution)/shard_map/reduce_scatter | solution.py:293
  1418.6 19.0 %reduce-scatter.42.cloned.1.call-done = bf16[96,128]{1,0:T(8,128)(2,1)} async-done(((bf16[384,128]{1,0:T(8,128)(2,1)}), bf16[96,128]{1,0:T(8,128)(2,1)}) %reduce-scatter.42.cloned.1.call-update) | async-done | bytes 24592 | tf_op jit(solution)/shard_map/reduce_scatter | solution.py:275
  1439.0 19.0 %reduce-scatter.40.cloned.1.call-done = bf16[96,128]{1,0:T(8,128)(2,1)} async-done(((bf16[384,128]{1,0:T(8,128)(2,1)}), bf16[96,128]{1,0:T(8,128)(2,1)}) %reduce-scatter.40.cloned.1.call-update) | async-done | bytes 24592 | tf_op jit(solution)/shard_map/reduce_scatter | solution.py:269
  1459.7 20.9 %reduce-scatter.38.cloned.1.call-done = bf16[96,768]{1,0:T(8,128)(2,1)} async-done(((bf16[384,768]{1,0:T(8,128)(2,1)}), bf16[96,768]{1,0:T(8,128)(2,1)}) %reduce-scatter.38.cloned.1.call-update) | async-done | bytes 147472 | tf_op jit(solution)/shard_map/reduce_scatter | solution.py:263
  1482.2 25.2 %reduce-scatter.36.cloned.1.call-done = f32[512,384]{1,0:T(8,128)} async-done(((f32[1024,384]{1,0:T(8,128)}), f32[512,384]{1,0:T(8,128)}) %reduce-scatter.36.cloned.1.call-update) | async-done | bytes 786448 | tf_op jit(solution)/shard_map/reduce_scatter | solution.py:68
  (220 shorter events, 329.2 us)
Async XLA Ops:
  7.2 130.1 %reduce-scatter.18.cloned.1.call-start = ((), (), s32[]{:S(2)}) async-start(), calls=%async_computation.17 | async-start | bytes 5242880 | tf_op jit(solution)/shard_map/reduce_scatter | solution.py:78
  94.7 82.0 %all-gather.11.cloned.1.call-start = ((), (), s32[]{:S(2)}) async-start(), calls=%async_computation.18 | async-start | bytes 1966080 | tf_op jit(solution)/shard_map/all_gather | solution.py:62
  156.7 89.9 %all-gather.19.cloned.1.call-start = ((), (), s32[]{:S(2)}) async-start(), calls=%async_computation.24 | async-start | bytes 4300800 | tf_op jit(solution)/shard_map/all_gather | solution.py:180
  157.4 116.6 %reduce-scatter.20.cloned.1.call-start = ((), (), s32[]{:S(2)}) async-start(), calls=%async_computation.19 | async-start | bytes 2359296 | tf_op jit(solution)/shard_map/reduce_scatter | solution.py:68
  180.3 163.6 %all-gather.13.cloned.1.call-start = ((), (), s32[]{:S(2)}) async-start(), calls=%async_computation.20 | async-start | bytes 4300800 | tf_op jit(solution)/shard_map/all_gather | solution.py:178
  180.8 231.3 %all-gather.15.cloned.1.call-start = ((), (), s32[]{:S(2)}) async-start(), calls=%async_computation.21 | async-start | bytes 4300800 | tf_op jit(solution)/shard_map/all_gather | solution.py:179
  181.4 366.6 %reduce-scatter.26.cloned.1.call-start = ((), (), s32[]{:S(2)}) async-start(), calls=%async_computation.26 | async-start | bytes 22937600 | tf_op jit(solution)/shard_map/reduce_scatter | solution.py:78
  257.6 544.3 %reduce-scatter.22.cloned.1.call-start = ((), (), s32[]{:S(2)}) async-start(), calls=%async_computation.22 | async-start | bytes 45875200 | tf_op jit(solution)/shard_map/reduce_scatter | solution.py:78
  439.0 433.6 %all-gather.21.cloned.1.call-start = ((), (), s32[]{:S(2)}) async-start(), calls=%async_computation.27 | async-start | bytes 11468800 | tf_op jit(solution)/shard_map/all_gather | solution.py:62
  809.7 127.0 %all-gather.23.cloned.1.call-start = ((), (), s32[]{:S(2)}) async-start(), calls=%async_computation.28 | async-start | bytes 11468800 | tf_op jit(solution)/shard_map/all_gather | solution.py:62
  810.3 190.8 %all-gather.17.cloned.1.call-start = ((), (), s32[]{:S(2)}) async-start(), calls=%async_computation.23 | async-start | bytes 11468800 | tf_op jit(solution)/shard_map/all_gather | solution.py:62
  811.1 218.9 %reduce-scatter.28.cloned.1.call-start = ((), (), s32[]{:S(2)}) async-start(), calls=%async_computation.29 | async-start | bytes 2359296 | tf_op jit(solution)/shard_map/reduce_scatter | solution.py:68
  946.5 112.5 %reduce-scatter.24.cloned.1.call-start = ((), (), s32[]{:S(2)}) async-start(), calls=%async_computation.25 | async-start | bytes 2359296 | tf_op jit(solution)/shard_map/reduce_scatter | solution.py:68
  1010.5 104.3 %reduce-scatter.30.cloned.1.call-start = ((), (), s32[]{:S(2)}) async-start(), calls=%async_computation.30 | async-start | bytes 3932160 | tf_op jit(solution)/shard_map/reduce_scatter | solution.py:78
  1076.7 92.3 %reduce-scatter.34.cloned.1.call-start = ((), (), s32[]{:S(2)}) async-start(), calls=%async_computation.33 | async-start | bytes 655360 | tf_op jit(solution)/shard_map/reduce_scatter | solution.py:238
  1132.0 58.6 %all-gather.25.cloned.1.call-start = ((), (), s32[]{:S(2)}) async-start(), calls=%async_computation.31 | async-start | bytes 1966080 | tf_op jit(solution)/shard_map/all_gather | solution.py:62
  1136.9 78.5 %reduce-scatter.44.cloned.1.call-start = ((), (), s32[]{:S(2)}) async-start(), calls=%async_computation.38 | async-start | bytes 737280 | tf_op jit(solution)/shard_map/reduce_scatter | solution.py:281
  1140.2 141.0 %reduce-scatter.48.cloned.1.call-start = ((), (), s32[]{:S(2)}) async-start(), calls=%async_computation.40 | async-start | bytes 4300800 | tf_op jit(solution)/shard_map/reduce_scatter | solution.py:290
  1149.4 199.1 %reduce-scatter.46.cloned.1.call-start = ((), (), s32[]{:S(2)}) async-start(), calls=%async_computation.39 | async-start | bytes 4300800 | tf_op jit(solution)/shard_map/reduce_scatter | solution.py:287
  1158.7 257.3 %reduce-scatter.50.cloned.1.call-start = ((), (), s32[]{:S(2)}) async-start(), calls=%async_computation.41 | async-start | bytes 4300800 | tf_op jit(solution)/shard_map/reduce_scatter | solution.py:293
  1169.0 268.7 %reduce-scatter.42.cloned.1.call-start = ((), (), s32[]{:S(2)}) async-start(), calls=%async_computation.37 | async-start | bytes 122880 | tf_op jit(solution)/shard_map/reduce_scatter | solution.py:275
  1185.9 272.1 %reduce-scatter.40.cloned.1.call-start = ((), (), s32[]{:S(2)}) async-start(), calls=%async_computation.36 | async-start | bytes 122880 | tf_op jit(solution)/shard_map/reduce_scatter | solution.py:269
  1187.1 293.5 %reduce-scatter.38.cloned.1.call-start = ((), (), s32[]{:S(2)}) async-start(), calls=%async_computation.35 | async-start | bytes 737280 | tf_op jit(solution)/shard_map/reduce_scatter | solution.py:263
  1193.7 313.8 %reduce-scatter.36.cloned.1.call-start = ((), (), s32[]{:S(2)}) async-start(), calls=%async_computation.34 | async-start | bytes 2359296 | tf_op jit(solution)/shard_map/reduce_scatter | solution.py:68
  (32 other events, 1418.3 us)
Sparse Core Ops, SparseCore 0:
  94.8 42.4 reduce-scatter.17
  156.8 19.8 all-gather.10
  178.2 68.2 all-gather.18
  249.3 24.7 reduce-scatter.19
  275.4 68.3 all-gather.12
  345.2 66.8 all-gather.14
  414.8 133.1 reduce-scatter.25
  550.6 251.2 reduce-scatter.21
  809.9 62.7 all-gather.20
  874.0 62.7 all-gather.22
  938.4 62.7 all-gather.16
  1003.8 26.1 reduce-scatter.27
  1032.8 26.1 reduce-scatter.23
  1076.9 37.8 reduce-scatter.29
  1121.0 21.6 reduce-scatter.33
  1145.6 21.6 reduce-scatter.31
  1169.3 21.2 all-gather.24
  1193.3 22.1 reduce-scatter.43
  1217.8 63.3 reduce-scatter.47
  1283.3 65.1 reduce-scatter.45
  1350.8 65.0 reduce-scatter.49
  1418.2 19.4 reduce-scatter.41
  1460.2 20.3 reduce-scatter.37
  1482.8 24.5 reduce-scatter.35
  (1 shorter events, 17.5 us)
where the time goes:
time: 1550 us; the launch traced here: 1540 us
  waiting for transfers between devices  1140 us (74%)
  blocking collectives  187 us (12%)
  matrix products  134 us (9%)
  other arithmetic  49.6 us (3%)
  between operations  18.9 us (1%)
    reduce_scatter x4, waiting for transfers between devices, width_sum(): lax.psum_scatter(term(jnp.int32(0), lax.axis_size('col') * (whole.shape[0...  442 us
    all_gather x5, waiting for transfers between devices, cols_whole(): lax.all_gather(shortened(local), 'col', axis=0, tiled=True)  176 us
    reduce_scatter x4, waiting for transfers between devices, rows_sum(): return lax.psum_scatter(term, 'row', scatter_dimension=0, tiled=True)  81.4 us
    all_gather x1, waiting for transfers between devices, shards(): lax.all_gather(w_up, 'dp', axis=0, tiled=True)  68.4 us
    reduce_scatter x1, waiting for transfers between devices, shards(): lax.psum_scatter(grad_down.astype(jnp.bfloat16), 'dp', scatter_dimension=...  65 us
    reduce_scatter x1, waiting for transfers between devices, shards(): lax.psum_scatter(grad_gate.astype(jnp.bfloat16), 'dp', scatter_dimension=...  64.8 us
    reduce_scatter x1, waiting for transfers between devices, shards(): lax.psum_scatter(grad_up.astype(jnp.bfloat16), 'dp', scatter_dimension=0,...  64.1 us
    all_gather x1, waiting for transfers between devices, shards(): lax.all_gather(w_down, 'dp', axis=0, tiled=True)  52.7 us
  transfers between devices with their start and end apart: 25, of which 23 were waited for; matrix products, arithmetic and copies ran while one was open for 10% of the time, Pallas kernels for 0%

commit v1 on v0

--- a/solution.py
+++ b/solution.py
@@ -7,6 +7,22 @@
 HEAD_SIZE = 128
 epsilon = 1e-06
 rope_base = 1000000.0
+
+
+def gather_around(x, axis, dim):
+    ways, here, step = (lax.axis_size(axis), lax.axis_index(axis), x.shape[dim])
+    lengths = [n * ways if d == dim else n for d, n in enumerate(x.shape)]
+    full = lax.dynamic_update_slice_in_dim(jnp.zeros(lengths, x.dtype), x, here * step, axis=dim)
+    going_up = going_down = x
+    for far in range(1, ways // 2 + 1):
+        going_up = lax.ppermute(going_up, axis, [(d, (d + 1) % ways) for d in range(ways)])
+        full = lax.dynamic_update_slice_in_dim(full, going_up, (here - far) % ways * step, axis=dim)
+        if 2 * far < ways:
+            going_down = lax.ppermute(going_down, axis, [(d, (d - 1) % ways) for d in range(ways)])
+            full = lax.dynamic_update_slice_in_dim(
+                full, going_down, (here + far) % ways * step, axis=dim
+            )
+    return full
 
 
 def shortened(shard):
@@ -177,7 +193,7 @@
         lax.all_gather(gain_mlp, "dp", axis=0, tiled=True),
         lax.all_gather(w_gate, "dp", axis=0, tiled=True),
         lax.all_gather(w_up, "dp", axis=0, tiled=True),
-        lax.all_gather(w_down, "dp", axis=0, tiled=True),
+        gather_around(w_down, "dp", 0),
     )
     local_rows = inputs.shape[0]
     seq_len = local_rows * lax.axis_size("row")

time: 1550 us -> 1450 us (0.935)
  waiting for transfers between devices: 1140 us -> 1020 us
  starting transfers between devices: 1.23 us -> 27 us
    ppermute x0 -> x3, waiting for transfers between devices: none -> 68.7 us  [the longest x2 53 us: gather_around(): lax.ppermute(going_up, axis, [(d, (d + 1) % ways) for d in range(ways)])]
    reduce_scatter x4, waiting for transfers between devices: 442 us -> 389 us  [width_sum(): lax.psum_scatter(term(jnp.int32(0), lax.axis_size('col') * (whole.shape[0...]
    all_gather x1 -> x0, waiting for transfers between devices: 52.7 us -> none  [shards(): lax.all_gather(w_down, 'dp', axis=0, tiled=True)]
    all_gather x1, waiting for transfers between devices: 51.1 us -> 0.01 us  [shards(): lax.all_gather(w_gate, 'dp', axis=0, tiled=True)]
    ppermute x0 -> x3, starting transfers between devices: none -> 25.4 us  [the longest x2 23 us: gather_around(): lax.ppermute(going_up, axis, [(d, (d + 1) % ways) for d in range(ways)])]
    all_gather x1, waiting for transfers between devices: 68.4 us -> 43.7 us  [shards(): lax.all_gather(w_up, 'dp', axis=0, tiled=True)]
  transfers between devices with their start and end apart: 25 -> 27, of which waited for: 23 -> 23; matrix products, arithmetic and copies ran while one was open for 10% -> 10% of each run, Pallas kernels for 0% -> 0%
where the time goes in v1:
time: 1450 us; the launch traced here: 1440 us
  waiting for transfers between devices  1020 us (70%)
  blocking collectives  183 us (13%)
  matrix products  121 us (8%)
  other arithmetic  51.8 us (4%)
  starting transfers between devices  27 us (2%)
  between operations  20.8 us (1%)
  local copies, waits for them, and re-layouts  15.7 us (1%)
    reduce_scatter x4, waiting for transfers between devices, width_sum(): lax.psum_scatter(term(jnp.int32(0), lax.axis_size('col') * (whole.shape[0...  389 us
    all_gather x5, waiting for transfers between devices, cols_whole(): lax.all_gather(shortened(local), 'col', axis=0, tiled=True)  180 us
    reduce_scatter x4, waiting for transfers between devices, rows_sum(): return lax.psum_scatter(term, 'row', scatter_dimension=0, tiled=True)  66.1 us
    reduce_scatter x1, waiting for transfers between devices, shards(): lax.psum_scatter(grad_down.astype(jnp.bfloat16), 'dp', scatter_dimension=...  64.8 us
    reduce_scatter x1, waiting for transfers between devices, shards(): lax.psum_scatter(grad_gate.astype(jnp.bfloat16), 'dp', scatter_dimension=...  64.8 us
    reduce_scatter x1, waiting for transfers between devices, shards(): lax.psum_scatter(grad_up.astype(jnp.bfloat16), 'dp', scatter_dimension=0,...  63.9 us
    ppermute x2, waiting for transfers between devices, gather_around(): lax.ppermute(going_up, axis, [(d, (d + 1) % ways) for d in range(ways)])  53 us
    all_gather x4, blocking collectives, rows_whole(): return lax.all_gather(local, 'row', axis=0, tiled=True)  43.8 us
  transfers between devices with their start and end apart: 27, of which 23 were waited for; matrix products, arithmetic and copies ran while one was open for 10% of the time, Pallas kernels for 0%

profile of v1, /device:TPU:0, one launch (start us, length us, event | category | flops | bytes accessed | tf_op | source)
XLA Modules:
  0.0 1436.2 jit_solution(2375159811167215295)
XLA Ops:
  48.8 16.3 %all_gather.74 = bf16[384,768]{1,0:T(8,128)(2,1)S(1)} all-gather(bf16[96,768]{1,0:T(8,128)(2,1)} %param.16), channel_id=1, replica_groups=mesh['dp'=4,'row'=2,'col'=4] {'dp'}, dimensions={0}, use_global_device_ids=true | all-gather | bytes 737280 | tf_op jit(solution)/shard_map/all_gather | solution.py:186
  97.6 41.1 %reduce-scatter.18.cloned.1.call-done = f32[256,1024]{0,1:T(8,128)} async-done(((f32[1024,1024]{0,1:T(8,128)}), f32[256,1024]{0,1:T(8,128)}) %reduce-scatter.18.cloned.1.call-update) | async-done | bytes 1048592 | tf_op jit(solution)/shard_map/reduce_scatter | solution.py:94
  157.5 17.3 %all_gather.83 = bf16[768,384]{1,0:T(8,128)(2,1)S(1)} all-gather(bf16[192,384]{1,0:T(8,128)(2,1)S(1)} %copy-done.31), channel_id=1, replica_groups=mesh['dp'=4,'row'=2,'col'=4] {'dp'}, dimensions={0}, use_global_device_ids=true | all-gather | bytes 737280 | tf_op jit(solution)/shard_map/all_gather | solution.py:192
  186.1 31.0 %collective-permute-done = bf16[1120,384]{1,0:T(8,128)(2,1)} collective-permute-done((bf16[1120,384]{1,0:T(8,128)(2,1)}, bf16[1120,384]{1,0:T(8,128)(2,1)}, u32[]{:S(2)}, u32[]{:S(2)}) %collective-permute-start) | collective-permute-done | bytes 860192 | tf_op jit(solution)/shard_map/ppermute | solution.py:18
  217.1 21.5 %collective-permute-start.2 = (bf16[1120,384]{1,0:T(8,128)(2,1)}, bf16[1120,384]{1,0:T(8,128)(2,1)}, u32[]{:S(2)}, u32[]{:S(2)}) collective-permute-start(bf16[1120,384]{1,0:T(8,128)(2,1)} %collective-permute-done), channel_id=1, source_target_pairs={{0,8},{8,16},{16,24},{24,0},{1,9},{9,17},{17,25},{25,1},{2,10},{10... | collective-permute-start | bytes 2580488 | tf_op jit(solution)/shard_map/ppermute | solution.py:18
  251.0 15.7 %collective-permute-done.1 = bf16[1120,384]{1,0:T(8,128)(2,1)} collective-permute-done((bf16[1120,384]{1,0:T(8,128)(2,1)}, bf16[1120,384]{1,0:T(8,128)(2,1)}, u32[]{:S(2)}, u32[]{:S(2)}) %collective-permute-start.1) | collective-permute-done | bytes 860192 | tf_op jit(solution)/shard_map/ppermute | solution.py:21
  268.1 22.0 %collective-permute-done.2 = bf16[1120,384]{1,0:T(8,128)(2,1)} collective-permute-done((bf16[1120,384]{1,0:T(8,128)(2,1)}, bf16[1120,384]{1,0:T(8,128)(2,1)}, u32[]{:S(2)}, u32[]{:S(2)}) %collective-permute-start.2) | collective-permute-done | bytes 860192 | tf_op jit(solution)/shard_map/ppermute | solution.py:18
  321.3 43.7 %all-gather.14.cloned.1.call-done = bf16[384,4480]{1,0:T(8,128)(2,1)} async-done(((bf16[96,4480]{1,0:T(8,128)(2,1)}), bf16[384,4480]{1,0:T(8,128)(2,1)}) %all-gather.14.cloned.1.call-update) | async-done | bytes 3440656 | tf_op jit(solution)/shard_map/all_gather | solution.py:195
  365.0 20.3 %fusion = f32[1024,8960]{1,0:T(8,128)} fusion(bf16[1024,384]{1,0:T(8,128)(2,1)} %all_gather.85, bf16[384,4480]{1,0:T(8,128)(2,1)} %all-gather.14.cloned.1.call-done, bf16[384,4480]{1,0:T(8,128)(2,1)} %all-gather.12.cloned.1.call-done), kind=kOutput, calls=%fused_computation.4 | convolution fusion | flops 7060193280 | bytes 44367872 | tf_op jit(solution)/shard_map/dot_general | solution.py:90
  385.3 56.1 %reduce-scatter.26.cloned.1.call-done = f32[256,4480]{1,0:T(8,128)} async-done(((f32[1024,4480]{1,0:T(8,128)}), f32[256,4480]{1,0:T(8,128)}) %reduce-scatter.26.cloned.1.call-update) | async-done | bytes 4587536 | tf_op jit(solution)/shard_map/reduce_scatter | solution.py:94
  441.4 253.7 %reduce-scatter.22.cloned.1.call-done = f32[256,8960]{1,0:T(8,128)} async-done(((f32[1024,8960]{1,0:T(8,128)}), f32[256,8960]{1,0:T(8,128)}) %reduce-scatter.22.cloned.1.call-update) | async-done | bytes 9175056 | tf_op jit(solution)/shard_map/reduce_scatter | solution.py:94
  704.7 61.2 %all-gather.18.cloned.1.call-done = bf16[1024,4480]{1,0:T(8,128)(2,1)} async-done(((bf16[256,4480]{1,0:T(8,128)(2,1)}), bf16[1024,4480]{1,0:T(8,128)(2,1)}) %all-gather.18.cloned.1.call-update) | async-done | bytes 9175056 | tf_op jit(solution)/shard_map/all_gather | solution.py:78
  775.3 54.9 %all-gather.20.cloned.1.call-done = bf16[1024,4480]{1,0:T(8,128)(2,1)} async-done(((bf16[256,4480]{1,0:T(8,128)(2,1)}), bf16[1024,4480]{1,0:T(8,128)(2,1)}) %all-gather.20.cloned.1.call-update) | async-done | bytes 9175056 | tf_op jit(solution)/shard_map/all_gather | solution.py:78
  839.9 54.6 %all-gather.16.cloned.1.call-done = bf16[1024,4480]{1,0:T(8,128)(2,1)} async-done(((bf16[256,4480]{1,0:T(8,128)(2,1)}), bf16[1024,4480]{1,0:T(8,128)(2,1)}) %all-gather.16.cloned.1.call-update) | async-done | bytes 9175056 | tf_op jit(solution)/shard_map/all_gather | solution.py:78
  903.3 20.2 %reduce-scatter.28.cloned.1.call-done = f32[512,384]{1,0:T(8,128)} async-done(((f32[1024,384]{1,0:T(8,128)}), f32[512,384]{1,0:T(8,128)}) %reduce-scatter.28.cloned.1.call-update) | async-done | bytes 786448 | tf_op jit(solution)/shard_map/reduce_scatter | solution.py:84
  931.6 20.8 %reduce-scatter.24.cloned.1.call-done = f32[512,384]{1,0:T(8,128)} async-done(((f32[1024,384]{1,0:T(8,128)}), f32[512,384]{1,0:T(8,128)}) %reduce-scatter.24.cloned.1.call-update) | async-done | bytes 786448 | tf_op jit(solution)/shard_map/reduce_scatter | solution.py:84
  970.3 38.0 %reduce-scatter.30.cloned.1.call-done = f32[256,768]{1,0:T(8,128)} async-done(((f32[1024,768]{1,0:T(8,128)}), f32[256,768]{1,0:T(8,128)}) %reduce-scatter.30.cloned.1.call-update) | async-done | bytes 786448 | tf_op jit(solution)/shard_map/reduce_scatter | solution.py:94
  1109.7 63.9 %reduce-scatter.48.cloned.1.call-done = bf16[96,4480]{1,0:T(8,128)(2,1)} async-done(((bf16[384,4480]{1,0:T(8,128)(2,1)}), bf16[96,4480]{1,0:T(8,128)(2,1)}) %reduce-scatter.48.cloned.1.call-update) | async-done | bytes 860176 | tf_op jit(solution)/shard_map/reduce_scatter | solution.py:306
  1176.1 64.8 %reduce-scatter.46.cloned.1.call-done = bf16[96,4480]{1,0:T(8,128)(2,1)} async-done(((bf16[384,4480]{1,0:T(8,128)(2,1)}), bf16[96,4480]{1,0:T(8,128)(2,1)}) %reduce-scatter.46.cloned.1.call-update) | async-done | bytes 860176 | tf_op jit(solution)/shard_map/reduce_scatter | solution.py:303
  1243.4 64.8 %reduce-scatter.50.cloned.1.call-done = bf16[1120,384]{1,0:T(8,128)(2,1)} async-done(((bf16[4480,384]{1,0:T(8,128)(2,1)}), bf16[1120,384]{1,0:T(8,128)(2,1)}) %reduce-scatter.50.cloned.1.call-update) | async-done | bytes 860176 | tf_op jit(solution)/shard_map/reduce_scatter | solution.py:309
  1310.9 19.1 %reduce-scatter.42.cloned.1.call-done = bf16[96,128]{1,0:T(8,128)(2,1)} async-done(((bf16[384,128]{1,0:T(8,128)(2,1)}), bf16[96,128]{1,0:T(8,128)(2,1)}) %reduce-scatter.42.cloned.1.call-update) | async-done | bytes 24592 | tf_op jit(solution)/shard_map/reduce_scatter | solution.py:291
  1331.4 18.9 %reduce-scatter.40.cloned.1.call-done = bf16[96,128]{1,0:T(8,128)(2,1)} async-done(((bf16[384,128]{1,0:T(8,128)(2,1)}), bf16[96,128]{1,0:T(8,128)(2,1)}) %reduce-scatter.40.cloned.1.call-update) | async-done | bytes 24592 | tf_op jit(solution)/shard_map/reduce_scatter | solution.py:285
  1353.3 19.6 %reduce-scatter.38.cloned.1.call-done = bf16[96,768]{1,0:T(8,128)(2,1)} async-done(((bf16[384,768]{1,0:T(8,128)(2,1)}), bf16[96,768]{1,0:T(8,128)(2,1)}) %reduce-scatter.38.cloned.1.call-update) | async-done | bytes 147472 | tf_op jit(solution)/shard_map/reduce_scatter | solution.py:279
  1374.6 25.1 %reduce-scatter.36.cloned.1.call-done = f32[512,384]{1,0:T(8,128)} async-done(((f32[1024,384]{1,0:T(8,128)}), f32[512,384]{1,0:T(8,128)}) %reduce-scatter.36.cloned.1.call-update) | async-done | bytes 786448 | tf_op jit(solution)/shard_map/reduce_scatter | solution.py:84
  (236 shorter events, 350.7 us)
Async XLA Ops:
  8.0 130.7 %reduce-scatter.18.cloned.1.call-start = ((), (), s32[]{:S(2)}) async-start(), calls=%async_computation.17 | async-start | bytes 5242880 | tf_op jit(solution)/shard_map/reduce_scatter | solution.py:94
  96.1 81.3 %all-gather.10.cloned.1.call-start = ((), (), s32[]{:S(2)}) async-start(), calls=%async_computation.18 | async-start | bytes 1966080 | tf_op jit(solution)/shard_map/all_gather | solution.py:78
  157.4 143.1 %reduce-scatter.20.cloned.1.call-start = ((), (), s32[]{:S(2)}) async-start(), calls=%async_computation.19 | async-start | bytes 2359296 | tf_op jit(solution)/shard_map/reduce_scatter | solution.py:84
  181.0 140.3 %all-gather.12.cloned.1.call-start = ((), (), s32[]{:S(2)}) async-start(), calls=%async_computation.20 | async-start | bytes 4300800 | tf_op jit(solution)/shard_map/all_gather | solution.py:194
  181.6 183.4 %all-gather.14.cloned.1.call-start = ((), (), s32[]{:S(2)}) async-start(), calls=%async_computation.21 | async-start | bytes 4300800 | tf_op jit(solution)/shard_map/all_gather | solution.py:195
  182.2 259.3 %reduce-scatter.26.cloned.1.call-start = ((), (), s32[]{:S(2)}) async-start(), calls=%async_computation.25 | async-start | bytes 22937600 | tf_op jit(solution)/shard_map/reduce_scatter | solution.py:94
  183.7 83.0 %collective-permute-start.1 = (bf16[1120,384]{1,0:T(8,128)(2,1)}, bf16[1120,384]{1,0:T(8,128)(2,1)}, u32[]{:S(2)}, u32[]{:S(2)}) collective-permute-start(bf16[1120,384]{1,0:T(8,128)(2,1)} %param.26), channel_id=1, source_target_pairs={{0,24},{8,0},{16,8},{24,16},{1,25},{9,1},{17,9},{25,17},{2,26},{10... | collective-permute-start | bytes 2580488 | tf_op jit(solution)/shard_map/ppermute | solution.py:21
  217.1 73.0 %collective-permute-start.2 = (bf16[1120,384]{1,0:T(8,128)(2,1)}, bf16[1120,384]{1,0:T(8,128)(2,1)}, u32[]{:S(2)}, u32[]{:S(2)}) collective-permute-start(bf16[1120,384]{1,0:T(8,128)(2,1)} %collective-permute-done), channel_id=1, source_target_pairs={{0,8},{8,16},{16,24},{24,0},{1,9},{9,17},{17,25},{25,1},{2,10},{10... | collective-permute-start | bytes 2580488 | tf_op jit(solution)/shard_map/ppermute | solution.py:18
  300.4 394.8 %reduce-scatter.22.cloned.1.call-start = ((), (), s32[]{:S(2)}) async-start(), calls=%async_computation.22 | async-start | bytes 45875200 | tf_op jit(solution)/shard_map/reduce_scatter | solution.py:94
  385.3 380.6 %all-gather.18.cloned.1.call-start = ((), (), s32[]{:S(2)}) async-start(), calls=%async_computation.26 | async-start | bytes 11468800 | tf_op jit(solution)/shard_map/all_gather | solution.py:78
  703.0 127.2 %all-gather.20.cloned.1.call-start = ((), (), s32[]{:S(2)}) async-start(), calls=%async_computation.27 | async-start | bytes 11468800 | tf_op jit(solution)/shard_map/all_gather | solution.py:78
  703.7 190.8 %all-gather.16.cloned.1.call-start = ((), (), s32[]{:S(2)}) async-start(), calls=%async_computation.23 | async-start | bytes 11468800 | tf_op jit(solution)/shard_map/all_gather | solution.py:78
  704.5 219.0 %reduce-scatter.28.cloned.1.call-start = ((), (), s32[]{:S(2)}) async-start(), calls=%async_computation.28 | async-start | bytes 2359296 | tf_op jit(solution)/shard_map/reduce_scatter | solution.py:84
  839.9 112.5 %reduce-scatter.24.cloned.1.call-start = ((), (), s32[]{:S(2)}) async-start(), calls=%async_computation.24 | async-start | bytes 2359296 | tf_op jit(solution)/shard_map/reduce_scatter | solution.py:84
  903.2 105.1 %reduce-scatter.30.cloned.1.call-start = ((), (), s32[]{:S(2)}) async-start(), calls=%async_computation.29 | async-start | bytes 3932160 | tf_op jit(solution)/shard_map/reduce_scatter | solution.py:94
  970.2 89.8 %reduce-scatter.34.cloned.1.call-start = ((), (), s32[]{:S(2)}) async-start(), calls=%async_computation.32 | async-start | bytes 655360 | tf_op jit(solution)/shard_map/reduce_scatter | solution.py:254
  1028.9 79.2 %reduce-scatter.44.cloned.1.call-start = ((), (), s32[]{:S(2)}) async-start(), calls=%async_computation.37 | async-start | bytes 737280 | tf_op jit(solution)/shard_map/reduce_scatter | solution.py:297
  1030.7 142.9 %reduce-scatter.48.cloned.1.call-start = ((), (), s32[]{:S(2)}) async-start(), calls=%async_computation.39 | async-start | bytes 4300800 | tf_op jit(solution)/shard_map/reduce_scatter | solution.py:306
  1039.8 201.1 %reduce-scatter.46.cloned.1.call-start = ((), (), s32[]{:S(2)}) async-start(), calls=%async_computation.38 | async-start | bytes 4300800 | tf_op jit(solution)/shard_map/reduce_scatter | solution.py:303
  1048.9 259.3 %reduce-scatter.50.cloned.1.call-start = ((), (), s32[]{:S(2)}) async-start(), calls=%async_computation.40 | async-start | bytes 4300800 | tf_op jit(solution)/shard_map/reduce_scatter | solution.py:309
  1060.0 270.1 %reduce-scatter.42.cloned.1.call-start = ((), (), s32[]{:S(2)}) async-start(), calls=%async_computation.36 | async-start | bytes 122880 | tf_op jit(solution)/shard_map/reduce_scatter | solution.py:291
  1075.3 275.0 %reduce-scatter.40.cloned.1.call-start = ((), (), s32[]{:S(2)}) async-start(), calls=%async_computation.35 | async-start | bytes 122880 | tf_op jit(solution)/shard_map/reduce_scatter | solution.py:285
  1076.5 296.5 %reduce-scatter.38.cloned.1.call-start = ((), (), s32[]{:S(2)}) async-start(), calls=%async_computation.34 | async-start | bytes 737280 | tf_op jit(solution)/shard_map/reduce_scatter | solution.py:279
  1086.4 313.3 %reduce-scatter.36.cloned.1.call-start = ((), (), s32[]{:S(2)}) async-start(), calls=%async_computation.33 | async-start | bytes 2359296 | tf_op jit(solution)/shard_map/reduce_scatter | solution.py:84
  (38 other events, 1045.7 us)
Sparse Core Ops, SparseCore 0:
  96.2 42.4 reduce-scatter.17
  157.5 19.8 all-gather.9
  181.1 26.1 reduce-scatter.19
  300.5 140.8 reduce-scatter.25
  443.9 251.2 reduce-scatter.21
  703.1 62.7 all-gather.17
  767.4 62.7 all-gather.19
  831.8 62.7 all-gather.15
  897.3 26.1 reduce-scatter.27
  926.2 26.1 reduce-scatter.23
  970.4 37.9 reduce-scatter.29
  1014.6 21.6 reduce-scatter.33
  1039.4 21.6 reduce-scatter.31
  1063.0 20.0 all-gather.21
  1085.8 22.1 reduce-scatter.43
  1110.2 63.3 reduce-scatter.47
  1175.8 65.0 reduce-scatter.45
  1243.1 65.0 reduce-scatter.49
  1310.5 19.5 reduce-scatter.41
  1332.7 17.5 reduce-scatter.39
  1352.6 20.2 reduce-scatter.37
  1375.2 24.4 reduce-scatter.35
Sparse Core Ops, SparseCore 1:
  183.0 115.0 all-gather.11
  299.5 65.4 all-gather.13
